TPU v7x, 128 devices: a whole 4x4x4 slice. The times are simulated.
128 devices in a mesh: tm: 16 (over y, x), row: 8 (over z, core).
Axes of the slice: x: 4, y: 4, z: 4, core: 2. Of those that a mesh axis runs over, the one named last changes fastest.
Arguments:
- starts: float32 [16, 8, 16384], P('tm', None, 'row'), may hold values from -6 to 6
- operator: float32 [16384, 16384], P('row', 'tm'), may hold values from -1 to 1
- coarse_left: float32 [16384, 256], P('row'), may hold values from -0.375 to 0.375
- coarse_right: float32 [16384, 256], P('row'), may hold values from -0.046875 to 0.046875
Outputs:
- new_ends: float32 [16, 8, 16384], P('tm', None, 'row')
All inputs are finite; a program needn't handle non-finite values.
Results may differ from a plain program's by a relative error of at most 0.00019.
Values sent between devices are 32-bit elements; how exact they have to be, the bound alone decides.
A program may use at most 64 MiB of HBM per device.

v0:
```python
import jax
import jax.numpy as jnp
from jax import lax
from jax.sharding import PartitionSpec as P

FINE = 4


highest = lax.Precision.HIGHEST


def laid_out(pieces, dim):
    pieces = jnp.moveaxis(pieces, 0, dim)
    lengths = pieces.shape
    return pieces.reshape(*lengths[:dim], lengths[dim] * lengths[dim + 1], *lengths[dim + 2 :])


def copy_for_each(array, axis):
    peers = lax.axis_size(axis)
    return lax.all_to_all(
        jnp.broadcast_to(array[None], (peers, *array.shape)), axis, 0, 0, tiled=True
    )


def gathered_copies(array, axis, dim):
    return laid_out(copy_for_each(array, axis), dim)


def broadcast(array, axis, root):
    return lax.dynamic_index_in_dim(lax.all_gather(array, axis), root, 0, keepdims=False)


def in_blocks(array, dim, peers):
    lengths = array.shape
    pieces = array.reshape(*lengths[:dim], peers, lengths[dim] // peers, *lengths[dim + 1 :])
    return jnp.moveaxis(pieces, dim, 0)


def sent_and_summed(array, axis, dim):
    peers = lax.axis_size(axis)
    pieces = lax.all_to_all(in_blocks(array, dim, peers), axis, 0, 0, tiled=True)
    return jnp.sum(pieces, axis=0)


def rows_for(lines, peers):
    spare = -len(lines) % peers
    return jnp.pad(lines, [(0, spare)] + [(0, 0)] * (lines.ndim - 1))


def nested_sum(array, axes):
    lines = array.reshape(-1, array.shape[-1])
    own = sent_and_summed(rows_for(lines, lax.axis_size(axes)), axes, 0)
    whole = gathered_copies(own, axes, 0)
    return whole[: len(lines)].reshape(array.shape)


def over_copies(array, axis):
    everything = copy_for_each(array, axis)
    return jnp.sum(everything, axis=0)


def together(arrays, axis):
    flat, at, outs = (jnp.concatenate([a.reshape(-1) for a in arrays]), 0, [])
    running = over_copies(flat, axis)
    for a in arrays:
        outs.append(running[at : at + a.size].reshape(a.shape))
        at += a.size
    return tuple(outs)


def combined_pairwise(pieces, combine):
    while len(jax.tree.leaves(pieces)[0]) > 1:
        pieces = jax.vmap(combine)(*(pieces[side::2] for side in (0, 1)))
    return pieces[0]


def prefix(array, axis, combine, identity):
    peers, place = (lax.axis_size(axis), lax.axis_index(axis))
    passed = jnp.arange(peers) < place

    def kept(part, zero, own):
        part = jnp.where(
            passed.reshape(-1, *(1 for _ in own.shape)), part, jnp.asarray(zero, own.dtype)
        )
        return part

    pieces = copy_for_each(array, axis)
    return combined_pairwise(kept(pieces, identity, array), combine)


def shifted(block, axis, distance):
    devices = range(lax.axis_size(axis))
    route = [(i - distance, i) for i in devices if i - distance in devices]
    return lax.ppermute(block, axis, route)


def project_rows(values, factor):
    return jnp.einsum("sen,nr->ser", values, factor, precision=highest)


def spread_rows(weights, factor):
    return jnp.einsum("ser,nr->sen", weights, factor, precision=highest)


def matmul(left_side, right_side):
    return jnp.dot(left_side, right_side, precision=highest, preferred_element_type=jnp.float32)


def times_columns(vectors, operator):
    return lax.dot_general(
        vectors,
        operator,
        (((1,), (1,)), ((), ())),
        precision=highest,
        preferred_element_type=jnp.float32,
    )


def walk_slices(zeta_run, total_run, kernel, defect_terms):
    total_run = total_run + zeta_run
    zeta_run = matmul(zeta_run, kernel) + defect_terms[0]
    records = [total_run]
    return (zeta_run, total_run, jnp.stack(records))


def local(starts, operator, coarse_left, coarse_right):
    local_slices = starts.shape[0]
    ensemble = starts.shape[1]
    rows_here = starts.shape[2]
    column_width = operator.shape[1]
    rank_width = coarse_right.shape[1]
    tm_count = lax.axis_size("tm")
    row_count = lax.axis_size("row")
    position = lax.axis_index("tm")
    step_time = 1.0 / (local_slices * tm_count)
    fine_time = step_time / FINE
    flattened = starts.reshape(local_slices * ensemble, rows_here)
    ratio_blocks = tm_count // row_count
    everyone = gathered_copies(flattened, "tm", 0)

    def fine_total(done_steps, current):
        column_piece = lax.dynamic_slice_in_dim(
            current, position % ratio_blocks * column_width, column_width, 1
        )
        columns = broadcast(column_piece, "row", position // ratio_blocks)
        images = nested_sum(times_columns(columns, operator), "tm")
        return current + fine_time * images

    everyone = lax.fori_loop(0, FINE, fine_total, everyone)
    fine_flat = lax.dynamic_slice_in_dim(
        everyone, position * flattened.shape[0], flattened.shape[0], 0
    )
    fine_ends = fine_flat.reshape(local_slices, ensemble, rows_here)
    old_projection = over_copies(project_rows(starts, coarse_right), "row")
    defects = fine_ends - (starts + step_time * spread_rows(old_projection, coarse_left))
    first_start = broadcast(starts[0], "tm", 0)
    defect_terms, cross_terms, first_terms = together(
        (
            project_rows(defects, coarse_right),
            matmul(coarse_left.T, coarse_right),
            matmul(first_start, coarse_right),
        ),
        "row",
    )
    kernel = jnp.eye(rank_width, dtype=jnp.float32) + step_time * cross_terms
    running = jnp.cumsum(defects, axis=0)
    before = prefix(running[-1], "tm", jnp.add, jnp.zeros_like(running[-1]))

    def reduced_turn(turn_index, carried):
        passing, totals = carried
        zeta_run, total_run, records = walk_slices(passing[0], passing[1], kernel, defect_terms)
        active = position == turn_index
        totals = jnp.where(active, records, totals)
        outgoing = jnp.where(active, jnp.stack([zeta_run, total_run]), passing)
        return (shifted(outgoing, "tm", 1), totals)

    entering = jnp.stack([first_terms, jnp.zeros_like(first_terms)])
    projected_sums = lax.fori_loop(
        0, tm_count, reduced_turn, (entering, jnp.zeros_like(defect_terms))
    )[1]
    new_ends = (
        first_start[None]
        + step_time * spread_rows(projected_sums, coarse_left)
        + before[None]
        + running
    )
    return new_ends


def solution(mesh):
    in_specs = (P("tm", None, "row"), P("row", "tm"), P("row", None), P("row", None))
    out_specs = P("tm", None, "row")
    return jax.shard_map(local, mesh=mesh, in_specs=in_specs, out_specs=out_specs, check_vma=False)
```

profile of v0, /device:TPU:8, one launch (start us, length us, event | category | flops | bytes accessed | tf_op | source)
XLA Modules:
  0.0 622.6 jit_solution(10763259418498421645)
XLA Ops:
  9.4 7.4 %all-to-all-start.2 = ((f32[16,8,2048]{2,1,0:T(8,128)}), f32[16,8,2048]{2,1,0:T(8,128)}, u32[]{:S(2)}, u32[]{:S(2)}) async-start(f32[16,8,2048]{2,1,0:T(8,128)} %broadcast_in_dim.49), calls=%async_computation.2 | async-start | bytes 2097152 | tf_op jit(solution)/shard_map/all_to_all | solution.py:20
  16.8 14.7 %all-to-all-done.2 = f32[16,8,2048]{2,1,0:T(8,128)} async-done(((f32[16,8,2048]{2,1,0:T(8,128)}), f32[16,8,2048]{2,1,0:T(8,128)}, u32[]{:S(2)}, u32[]{:S(2)}) %all-to-all-start.2) | async-done | bytes 1048608 | tf_op jit(solution)/shard_map/all_to_all | solution.py:20
  31.5 361.1 %while.31 = (s32[]{:T(128)}, f32[128,2048]{1,0:T(8,128)}, s32[]{:T(128)}, s32[]{:T(128)}, f32[2048,1024]{1,0:T(8,128)}, /*index=5*/s32[]{:T(128)}, f32[]{:T(128)}) while((s32[]{:T(128)}, f32[128,2048]{1,0:T(8,128)}, s32[]{:T(128)}, s32[]{:T(128)}, f32[2048,1024]{1,0:T(8,128)}, /*index=5*/s32[]{:T(128)}, f32[]{:T(128)}) %tuple.67), condition=%wide.region_2.3_spmd, body=%wide.region_0.2_spmd.sunk | while | flops 3221995520 | bytes 35783324 | solution.py:149
  33.5 33.7 %all-gather.8.cloned.1.call-done = f32[1024,1024]{1,0:T(8,128)} async-done(((f32[128,1024]{1,0:T(8,128)}), f32[1024,1024]{1,0:T(8,128)}) %all-gather.8.cloned.1.call-update) | async-done | bytes 4194320 | tf_op jit(solution)/shard_map/while/body/eval_jaxpr/all_gather | solution.py:30
  67.1 11.2 %fusion.42 = f32[16,8,2048]{2,1,0:T(8,128)S(1)} fusion(f32[2048,1024]{1,0:T(8,128)} %get-tuple-element.525, f32[8,128,1024]{2,1,0:T(8,128)} %bitcast.78, s32[]{:T(128)} %get-tuple-element.524), kind=kOutput, calls=%fused_computation.clone.1 | convolution fusion | flops 3221225472 | bytes 9961984 | tf_op jit(solution)/shard_map/while/body/eval_jaxpr/dot_general | solution.py:110
  78.3 22.0 %all_to_all.41 = f32[16,8,2048]{2,1,0:T(8,128)S(1)} all-to-all(f32[16,8,2048]{2,1,0:T(8,128)S(1)} %fusion.42), channel_id=1, replica_groups=mesh['tm'=16,'row'=8] {'tm'}, dimensions={0} | all-to-all | bytes 2097152 | tf_op jit(solution)/shard_map/while/body/eval_jaxpr/all_to_all | solution.py:41
  101.5 6.1 all-to-all-start.1
  107.6 13.9 %all-to-all-done.1 = f32[16,8,2048]{2,1,0:T(8,128)S(1)} async-done(((f32[16,8,2048]{2,1,0:T(8,128)}), f32[16,8,2048]{2,1,0:T(8,128)S(1)}, u32[]{:S(2)}, u32[]{:S(2)}) %all-to-all-start.1) | async-done | bytes 1048608 | tf_op jit(solution)/shard_map/while/body/eval_jaxpr/all_to_all | solution.py:20
  125.7 31.2 %all-gather.8.cloned.1.call-done = f32[1024,1024]{1,0:T(8,128)} async-done(((f32[128,1024]{1,0:T(8,128)}), f32[1024,1024]{1,0:T(8,128)}) %all-gather.8.cloned.1.call-update) | async-done | bytes 4194320 | tf_op jit(solution)/shard_map/while/body/eval_jaxpr/all_gather | solution.py:30
  156.9 11.1 %fusion.42 = f32[16,8,2048]{2,1,0:T(8,128)S(1)} fusion(f32[2048,1024]{1,0:T(8,128)} %get-tuple-element.525, f32[8,128,1024]{2,1,0:T(8,128)} %bitcast.78, s32[]{:T(128)} %get-tuple-element.524), kind=kOutput, calls=%fused_computation.clone.1 | convolution fusion | flops 3221225472 | bytes 9961984 | tf_op jit(solution)/shard_map/while/body/eval_jaxpr/dot_general | solution.py:110
  168.0 22.0 %all_to_all.41 = f32[16,8,2048]{2,1,0:T(8,128)S(1)} all-to-all(f32[16,8,2048]{2,1,0:T(8,128)S(1)} %fusion.42), channel_id=1, replica_groups=mesh['tm'=16,'row'=8] {'tm'}, dimensions={0} | all-to-all | bytes 2097152 | tf_op jit(solution)/shard_map/while/body/eval_jaxpr/all_to_all | solution.py:41
  197.3 13.8 %all-to-all-done.1 = f32[16,8,2048]{2,1,0:T(8,128)S(1)} async-done(((f32[16,8,2048]{2,1,0:T(8,128)}), f32[16,8,2048]{2,1,0:T(8,128)S(1)}, u32[]{:S(2)}, u32[]{:S(2)}) %all-to-all-start.1) | async-done | bytes 1048608 | tf_op jit(solution)/shard_map/while/body/eval_jaxpr/all_to_all | solution.py:20
  215.4 31.2 %all-gather.8.cloned.1.call-done = f32[1024,1024]{1,0:T(8,128)} async-done(((f32[128,1024]{1,0:T(8,128)}), f32[1024,1024]{1,0:T(8,128)}) %all-gather.8.cloned.1.call-update) | async-done | bytes 4194320 | tf_op jit(solution)/shard_map/while/body/eval_jaxpr/all_gather | solution.py:30
  246.6 11.2 %fusion.42 = f32[16,8,2048]{2,1,0:T(8,128)S(1)} fusion(f32[2048,1024]{1,0:T(8,128)} %get-tuple-element.525, f32[8,128,1024]{2,1,0:T(8,128)} %bitcast.78, s32[]{:T(128)} %get-tuple-element.524), kind=kOutput, calls=%fused_computation.clone.1 | convolution fusion | flops 3221225472 | bytes 9961984 | tf_op jit(solution)/shard_map/while/body/eval_jaxpr/dot_general | solution.py:110
  257.7 22.0 %all_to_all.41 = f32[16,8,2048]{2,1,0:T(8,128)S(1)} all-to-all(f32[16,8,2048]{2,1,0:T(8,128)S(1)} %fusion.42), channel_id=1, replica_groups=mesh['tm'=16,'row'=8] {'tm'}, dimensions={0} | all-to-all | bytes 2097152 | tf_op jit(solution)/shard_map/while/body/eval_jaxpr/all_to_all | solution.py:41
  287.0 13.9 %all-to-all-done.1 = f32[16,8,2048]{2,1,0:T(8,128)S(1)} async-done(((f32[16,8,2048]{2,1,0:T(8,128)}), f32[16,8,2048]{2,1,0:T(8,128)S(1)}, u32[]{:S(2)}, u32[]{:S(2)}) %all-to-all-start.1) | async-done | bytes 1048608 | tf_op jit(solution)/shard_map/while/body/eval_jaxpr/all_to_all | solution.py:20
  305.1 30.8 %all-gather.8.cloned.1.call-done = f32[1024,1024]{1,0:T(8,128)} async-done(((f32[128,1024]{1,0:T(8,128)}), f32[1024,1024]{1,0:T(8,128)}) %all-gather.8.cloned.1.call-update) | async-done | bytes 4194320 | tf_op jit(solution)/shard_map/while/body/eval_jaxpr/all_gather | solution.py:30
  336.0 11.2 %fusion.42 = f32[16,8,2048]{2,1,0:T(8,128)S(1)} fusion(f32[2048,1024]{1,0:T(8,128)} %get-tuple-element.525, f32[8,128,1024]{2,1,0:T(8,128)} %bitcast.78, s32[]{:T(128)} %get-tuple-element.524), kind=kOutput, calls=%fused_computation.clone.1 | convolution fusion | flops 3221225472 | bytes 9961984 | tf_op jit(solution)/shard_map/while/body/eval_jaxpr/dot_general | solution.py:110
  347.1 22.0 %all_to_all.41 = f32[16,8,2048]{2,1,0:T(8,128)S(1)} all-to-all(f32[16,8,2048]{2,1,0:T(8,128)S(1)} %fusion.42), channel_id=1, replica_groups=mesh['tm'=16,'row'=8] {'tm'}, dimensions={0} | all-to-all | bytes 2097152 | tf_op jit(solution)/shard_map/while/body/eval_jaxpr/all_to_all | solution.py:41
  376.4 13.9 %all-to-all-done.1 = f32[16,8,2048]{2,1,0:T(8,128)S(1)} async-done(((f32[16,8,2048]{2,1,0:T(8,128)}), f32[16,8,2048]{2,1,0:T(8,128)S(1)}, u32[]{:S(2)}, u32[]{:S(2)}) %all-to-all-start.1) | async-done | bytes 1048608 | tf_op jit(solution)/shard_map/while/body/eval_jaxpr/all_to_all | solution.py:20
  410.7 6.6 %all-to-all-start.5 = ((f32[16,8,2048]{2,1,0:T(8,128)}), f32[16,8,2048]{2,1,0:T(8,128)S(1)}, u32[]{:S(2)}, u32[]{:S(2)}) async-start(f32[16,8,2048]{2,1,0:T(8,128)} %broadcast_in_dim.53), calls=%async_computation.5 | async-start | bytes 2097152 | tf_op jit(solution)/shard_map/all_to_all | solution.py:20
  417.3 24.0 %all-gather.6.cloned.1.call-done = f32[16,8,2048]{2,1,0:T(8,128)} async-done(((f32[1,8,2048]{2,1,0:T(8,128)}), f32[16,8,2048]{2,1,0:T(8,128)}) %all-gather.6.cloned.1.call-update) | async-done | bytes 1048592 | tf_op jit(solution)/shard_map/all_gather | solution.py:30
  452.2 28.1 %all-to-all-done.4 = f32[8,1,69632]{2,1,0:T(1,128)} async-done(((f32[8,1,69632]{2,1,0:T(1,128)}), f32[8,1,69632]{2,1,0:T(1,128)}, u32[]{:S(2)}, u32[]{:S(2)}) %all-to-all-start.4) | async-done | bytes 2228256 | tf_op jit(solution)/shard_map/all_to_all | solution.py:20
  484.3 127.9 %while.32 = (s32[]{:T(128)}, f32[2,8,256]{2,1,0:T(8,128)S(1)}, f32[1,8,256]{2,1,0:T(8,128)S(1)}, s32[]{:T(128)}, f32[256,256]{1,0:T(8,128)S(1)}, /*index=5*/f32[...) while((s32[]{:T(128)}, f32[2,8,256]{2,1,0:T(8,128)S(1)}, ...), condition=%wide.wide.region_6.7_spmd.clone, body=%wide.wide.region_5.6_spmd.clone.sunk | while | flops 6307844 | bytes 442522 | solution.py:178
  (150 shorter events, 205.5 us)
Async XLA Ops:
  9.4 22.1 %all-to-all-start.2 = ((f32[16,8,2048]{2,1,0:T(8,128)}), f32[16,8,2048]{2,1,0:T(8,128)}, u32[]{:S(2)}, u32[]{:S(2)}) async-start(f32[16,8,2048]{2,1,0:T(8,128)} %broadcast_in_dim.49), calls=%async_computation.2 | async-start | bytes 2097152 | tf_op jit(solution)/shard_map/all_to_all | solution.py:20
  31.5 35.6 %all-gather.8.cloned.1.call-start = ((), (), s32[]{:S(2)}) async-start(), calls=%async_computation.7 | async-start | bytes 4718592 | tf_op jit(solution)/shard_map/while/body/eval_jaxpr/all_gather | solution.py:30
  101.5 20.0 %all-to-all-start.1 = ((f32[16,8,2048]{2,1,0:T(8,128)}), f32[16,8,2048]{2,1,0:T(8,128)S(1)}, u32[]{:S(2)}, u32[]{:S(2)}) async-start(f32[16,8,2048]{2,1,0:T(8,128)} %broadcast_in_dim.58), calls=%async_computation.1 | async-start | bytes 2097152 | tf_op jit(solution)/shard_map/while/body/eval_jaxpr/all_to_all | solution.py:20
  123.8 33.1 %all-gather.8.cloned.1.call-start = ((), (), s32[]{:S(2)}) async-start(), calls=%async_computation.7 | async-start | bytes 4718592 | tf_op jit(solution)/shard_map/while/body/eval_jaxpr/all_gather | solution.py:30
  191.2 20.0 %all-to-all-start.1 = ((f32[16,8,2048]{2,1,0:T(8,128)}), f32[16,8,2048]{2,1,0:T(8,128)S(1)}, u32[]{:S(2)}, u32[]{:S(2)}) async-start(f32[16,8,2048]{2,1,0:T(8,128)} %broadcast_in_dim.58), calls=%async_computation.1 | async-start | bytes 2097152 | tf_op jit(solution)/shard_map/while/body/eval_jaxpr/all_to_all | solution.py:20
  213.5 33.1 %all-gather.8.cloned.1.call-start = ((), (), s32[]{:S(2)}) async-start(), calls=%async_computation.7 | async-start | bytes 4718592 | tf_op jit(solution)/shard_map/while/body/eval_jaxpr/all_gather | solution.py:30
  280.9 20.0 %all-to-all-start.1 = ((f32[16,8,2048]{2,1,0:T(8,128)}), f32[16,8,2048]{2,1,0:T(8,128)S(1)}, u32[]{:S(2)}, u32[]{:S(2)}) async-start(f32[16,8,2048]{2,1,0:T(8,128)} %broadcast_in_dim.58), calls=%async_computation.1 | async-start | bytes 2097152 | tf_op jit(solution)/shard_map/while/body/eval_jaxpr/all_to_all | solution.py:20
  303.2 32.8 %all-gather.8.cloned.1.call-start = ((), (), s32[]{:S(2)}) async-start(), calls=%async_computation.7 | async-start | bytes 4718592 | tf_op jit(solution)/shard_map/while/body/eval_jaxpr/all_gather | solution.py:30
  370.3 20.0 %all-to-all-start.1 = ((f32[16,8,2048]{2,1,0:T(8,128)}), f32[16,8,2048]{2,1,0:T(8,128)S(1)}, u32[]{:S(2)}, u32[]{:S(2)}) async-start(f32[16,8,2048]{2,1,0:T(8,128)} %broadcast_in_dim.58), calls=%async_computation.1 | async-start | bytes 2097152 | tf_op jit(solution)/shard_map/while/body/eval_jaxpr/all_to_all | solution.py:20
  392.6 48.7 %all-gather.6.cloned.1.call-start = ((), (), s32[]{:S(2)}) async-start(), calls=%async_computation.6 | async-start | bytes 1114112 | tf_op jit(solution)/shard_map/all_gather | solution.py:30
  396.4 9.5 %all-to-all-start.3 = ((f32[8,1,8,256]{3,2,1,0:T(8,128)}), f32[8,1,8,256]{3,2,1,0:T(8,128)S(1)}, u32[]{:S(2)}, u32[]{:S(2)}) async-start(f32[8,1,8,256]{3,2,1,0:T(8,128)} %broadcast_in_dim.50), calls=%async_computation.3 | async-start | bytes 131072 | tf_op jit(solution)/shard_map/all_to_all | solution.py:20
  410.7 34.1 %all-to-all-start.5 = ((f32[16,8,2048]{2,1,0:T(8,128)}), f32[16,8,2048]{2,1,0:T(8,128)S(1)}, u32[]{:S(2)}, u32[]{:S(2)}) async-start(f32[16,8,2048]{2,1,0:T(8,128)} %broadcast_in_dim.53), calls=%async_computation.5 | async-start | bytes 2097152 | tf_op jit(solution)/shard_map/all_to_all | solution.py:20
  447.4 33.0 %all-to-all-start.4 = ((f32[8,1,69632]{2,1,0:T(1,128)}), f32[8,1,69632]{2,1,0:T(1,128)}, u32[]{:S(2)}, u32[]{:S(2)}) async-start(f32[8,1,69632]{2,1,0:T(1,128)} %broadcast_in_dim.51), calls=%async_computation.4 | async-start | bytes 4456448 | tf_op jit(solution)/shard_map/all_to_all | solution.py:20
  484.5 7.7 %collective-permute-start = (f32[2,8,256]{2,1,0:T(8,128)S(1)}, f32[2,8,256]{2,1,0:T(8,128)S(1)}, u32[]{:S(2)}, u32[]{:S(2)}) collective-permute-start(f32[2,8,256]{2,1,0:T(8,128)S(1)} %maximum_select_fusion.3), channel_id=1, source_target_pairs={{0,8},{8,16},{16,24},{24,32},{32,40},{40,48},{48,56},{56,64},{64,7... | collective-permute-start | bytes 49160 | tf_op jit(solution)/shard_map/while/body/eval_jaxpr/ppermute | solution.py:94
  492.5 7.7 %collective-permute-start = (f32[2,8,256]{2,1,0:T(8,128)S(1)}, f32[2,8,256]{2,1,0:T(8,128)S(1)}, u32[]{:S(2)}, u32[]{:S(2)}) collective-permute-start(f32[2,8,256]{2,1,0:T(8,128)S(1)} %maximum_select_fusion.3), channel_id=1, source_target_pairs={{0,8},{8,16},{16,24},{24,32},{32,40},{40,48},{48,56},{56,64},{64,7... | collective-permute-start | bytes 49160 | tf_op jit(solution)/shard_map/while/body/eval_jaxpr/ppermute | solution.py:94
  500.5 7.7 %collective-permute-start = (f32[2,8,256]{2,1,0:T(8,128)S(1)}, f32[2,8,256]{2,1,0:T(8,128)S(1)}, u32[]{:S(2)}, u32[]{:S(2)}) collective-permute-start(f32[2,8,256]{2,1,0:T(8,128)S(1)} %maximum_select_fusion.3), channel_id=1, source_target_pairs={{0,8},{8,16},{16,24},{24,32},{32,40},{40,48},{48,56},{56,64},{64,7... | collective-permute-start | bytes 49160 | tf_op jit(solution)/shard_map/while/body/eval_jaxpr/ppermute | solution.py:94
  508.5 7.7 %collective-permute-start = (f32[2,8,256]{2,1,0:T(8,128)S(1)}, f32[2,8,256]{2,1,0:T(8,128)S(1)}, u32[]{:S(2)}, u32[]{:S(2)}) collective-permute-start(f32[2,8,256]{2,1,0:T(8,128)S(1)} %maximum_select_fusion.3), channel_id=1, source_target_pairs={{0,8},{8,16},{16,24},{24,32},{32,40},{40,48},{48,56},{56,64},{64,7... | collective-permute-start | bytes 49160 | tf_op jit(solution)/shard_map/while/body/eval_jaxpr/ppermute | solution.py:94
  516.5 7.7 %collective-permute-start = (f32[2,8,256]{2,1,0:T(8,128)S(1)}, f32[2,8,256]{2,1,0:T(8,128)S(1)}, u32[]{:S(2)}, u32[]{:S(2)}) collective-permute-start(f32[2,8,256]{2,1,0:T(8,128)S(1)} %maximum_select_fusion.3), channel_id=1, source_target_pairs={{0,8},{8,16},{16,24},{24,32},{32,40},{40,48},{48,56},{56,64},{64,7... | collective-permute-start | bytes 49160 | tf_op jit(solution)/shard_map/while/body/eval_jaxpr/ppermute | solution.py:94
  524.5 7.7 %collective-permute-start = (f32[2,8,256]{2,1,0:T(8,128)S(1)}, f32[2,8,256]{2,1,0:T(8,128)S(1)}, u32[]{:S(2)}, u32[]{:S(2)}) collective-permute-start(f32[2,8,256]{2,1,0:T(8,128)S(1)} %maximum_select_fusion.3), channel_id=1, source_target_pairs={{0,8},{8,16},{16,24},{24,32},{32,40},{40,48},{48,56},{56,64},{64,7... | collective-permute-start | bytes 49160 | tf_op jit(solution)/shard_map/while/body/eval_jaxpr/ppermute | solution.py:94
  540.5 7.7 %collective-permute-start = (f32[2,8,256]{2,1,0:T(8,128)S(1)}, f32[2,8,256]{2,1,0:T(8,128)S(1)}, u32[]{:S(2)}, u32[]{:S(2)}) collective-permute-start(f32[2,8,256]{2,1,0:T(8,128)S(1)} %maximum_select_fusion.3), channel_id=1, source_target_pairs={{0,8},{8,16},{16,24},{24,32},{32,40},{40,48},{48,56},{56,64},{64,7... | collective-permute-start | bytes 49160 | tf_op jit(solution)/shard_map/while/body/eval_jaxpr/ppermute | solution.py:94
  556.5 7.7 %collective-permute-start = (f32[2,8,256]{2,1,0:T(8,128)S(1)}, f32[2,8,256]{2,1,0:T(8,128)S(1)}, u32[]{:S(2)}, u32[]{:S(2)}) collective-permute-start(f32[2,8,256]{2,1,0:T(8,128)S(1)} %maximum_select_fusion.3), channel_id=1, source_target_pairs={{0,8},{8,16},{16,24},{24,32},{32,40},{40,48},{48,56},{56,64},{64,7... | collective-permute-start | bytes 49160 | tf_op jit(solution)/shard_map/while/body/eval_jaxpr/ppermute | solution.py:94
  572.4 7.7 %collective-permute-start = (f32[2,8,256]{2,1,0:T(8,128)S(1)}, f32[2,8,256]{2,1,0:T(8,128)S(1)}, u32[]{:S(2)}, u32[]{:S(2)}) collective-permute-start(f32[2,8,256]{2,1,0:T(8,128)S(1)} %maximum_select_fusion.3), channel_id=1, source_target_pairs={{0,8},{8,16},{16,24},{24,32},{32,40},{40,48},{48,56},{56,64},{64,7... | collective-permute-start | bytes 49160 | tf_op jit(solution)/shard_map/while/body/eval_jaxpr/ppermute | solution.py:94
  588.4 7.7 %collective-permute-start = (f32[2,8,256]{2,1,0:T(8,128)S(1)}, f32[2,8,256]{2,1,0:T(8,128)S(1)}, u32[]{:S(2)}, u32[]{:S(2)}) collective-permute-start(f32[2,8,256]{2,1,0:T(8,128)S(1)} %maximum_select_fusion.3), channel_id=1, source_target_pairs={{0,8},{8,16},{16,24},{24,32},{32,40},{40,48},{48,56},{56,64},{64,7... | collective-permute-start | bytes 49160 | tf_op jit(solution)/shard_map/while/body/eval_jaxpr/ppermute | solution.py:94
  604.4 7.7 %collective-permute-start = (f32[2,8,256]{2,1,0:T(8,128)S(1)}, f32[2,8,256]{2,1,0:T(8,128)S(1)}, u32[]{:S(2)}, u32[]{:S(2)}) collective-permute-start(f32[2,8,256]{2,1,0:T(8,128)S(1)} %maximum_select_fusion.3), channel_id=1, source_target_pairs={{0,8},{8,16},{16,24},{24,32},{32,40},{40,48},{48,56},{56,64},{64,7... | collective-permute-start | bytes 49160 | tf_op jit(solution)/shard_map/while/body/eval_jaxpr/ppermute | solution.py:94
  (9 other events, 796.4 us)
Sparse Core Ops, SparseCore 0:
  34.0 33.0 all-gather.7
  126.3 30.5 all-gather.7
  216.0 30.5 all-gather.7
  305.4 30.5 all-gather.7
Sparse Core Ops, SparseCore 1:
  395.2 46.0 all-gather.5
where the time goes:
time: 624 us; the launch traced here: 623 us
  waiting for transfers between devices  342 us (55%)
  blocking collectives  88.1 us (14%)
  starting transfers between devices  77.9 us (12%)
  matrix products  64.7 us (10%)
  local copies, waits for them, and re-layouts  19.6 us (3%)
  other arithmetic  14.9 us (2%)
  between operations  14.7 us (2%)
    all_gather x5, waiting for transfers between devices, broadcast(): lax.all_gather(array, axis)  151 us
    all_to_all x8, waiting for transfers between devices, copy_for_each(): lax.all_to_all(jnp.broadcast_to(array[None], (peers, *array.shape)), axis...  98.2 us
    ppermute x16, waiting for transfers between devices, shifted(): return lax.ppermute(block, axis, route)  92.5 us
    all_to_all x4, blocking collectives, sent_and_summed(): lax.all_to_all(in_blocks(array, dim, peers), axis, 0, 0, tiled=True)  88.1 us
    all_to_all x8, starting transfers between devices, copy_for_each(): lax.all_to_all(jnp.broadcast_to(array[None], (peers, *array.shape)), axis...  46.6 us
    dot_general x4, matrix products, times_columns(): lax.dot_general(vectors, operator, (((1,), (1,)), ((), ())), precision=hi...  44.6 us
    ppermute x16, starting transfers between devices, shifted(): return lax.ppermute(block, axis, route)  31.2 us
  transfers between devices with their start and end apart: 29, of which 27 were waited for; matrix products, arithmetic and copies ran while one was open for 3% of the time, Pallas kernels for 0%

commit v1 on v0

v1 whole, which is shorter than its diff:
```python
import functools

import jax
import jax.numpy as jnp
from jax import lax
from jax.experimental import pallas as pl
from jax.experimental.pallas import tpu as pltpu
from jax.sharding import PartitionSpec as P

MESH = pl.DeviceIdType.MESH
F32 = jnp.float32
BF16 = jnp.bfloat16
HIGHEST = lax.Precision.HIGHEST

FINE = 4
SLICES = 16
E = 8
LANES = SLICES * E
STEP_TIME = 1.0 / SLICES
FINE_TIME = STEP_TIME / FINE
BLK = 256


def split(values):
    high = values.astype(BF16)
    low = (values - high.astype(F32)).astype(BF16)
    return high, low


def dot(left, right):
    return jnp.dot(left, right, preferred_element_type=F32)


def exact(left, right):
    return jnp.dot(left, right, precision=HIGHEST, preferred_element_type=F32)


def kernel(
    starts_hbm, a_hbm, l_hbm, r_hbm, out_ref,
    starts_v, next_v, a_st, a_hi, a_lo, l_v, r_v, r_hi, r_lo, lt_hi, lt_lo,
    p0, xb, xx, qb, p1, sb, p2, qf, fx, fs, fy,
    gpart, grs, gown, gmat, kpow, hpart, hrow, hown, hall, scan,
    load_sem, next_sem, p0_ss, p0_rs, p1_ss, p1_rs, p2_ss, p2_rs, x_ss, xp_ss, x_rs,
    fx_ss, fx_rs, fy_ss, fy_rs, g1_ss, g1_rs, g2_ss, g2_rs, h1_ss, h1_rs, h2_ss, h2_rs,
):
    tm = lax.axis_index("tm")
    row = lax.axis_index("row")
    x, y = tm % 4, tm // 4
    z, c = row // 2, row % 2
    home = (x // 2) == c
    diagonal = y == z

    def at(xx_, yy_, zz_, cc_):
        return (yy_ * 4 + xx_, zz_ * 2 + cc_)

    def rcopy(src, dst, ss, rs, device):
        return pltpu.make_async_remote_copy(
            src_ref=src, dst_ref=dst, send_sem=ss, recv_sem=rs, device_id=device, device_id_type=MESH
        )

    me = (tm, row)

    def arrived(dst, ss, rs):
        rcopy(dst, dst, ss, rs, me).wait_recv()

    chunks = a_st.shape[0]
    rows_a = a_st.shape[1]

    def load_a(i):
        return pltpu.make_async_copy(a_hbm.at[pl.ds(i * rows_a, rows_a), :], a_st.at[i], load_sem.at[3 + i])

    load_starts = pltpu.make_async_copy(starts_hbm.at[0], starts_v, load_sem.at[0])
    load_l = pltpu.make_async_copy(l_hbm, l_v, load_sem.at[1])
    load_r = pltpu.make_async_copy(r_hbm, r_v, load_sem.at[2])
    load_starts.start()
    for i in range(chunks):
        load_a(i).start()
    load_l.start()
    load_r.start()

    barrier = pltpu.get_barrier_semaphore()

    def hello(device):
        pl.semaphore_signal(barrier, inc=1, device_id=device, device_id_type=MESH)

    for d in range(1, 16):
        hello(((tm + d) % 16, row))
    for d in range(1, 8):
        hello((tm, (row + d) % 8))

    @pl.when(home)
    def _():
        for t in range(16):
            other = (t, y * 2 + c)

            @pl.when(jnp.logical_not((tm == t) & diagonal))
            def _():
                hello(other)

    own_target = (home & diagonal).astype(jnp.int32)
    pl.semaphore_wait(barrier, 15 + 7 + 8 - own_target)

    load_starts.wait()

    def p0_copy(i):
        h, zz = i // 4, i % 4
        return rcopy(
            starts_v.at[:, pl.ds(pl.multiple_of(i * BLK, BLK), BLK)], p0.at[tm], p0_ss.at[i], p0_rs.at[tm],
            at(2 * c + h, z, zz, c),
        )

    def p0_self(i):
        return home & diagonal & (i // 4 == x % 2) & (i % 4 == z)

    for i in range(8):
        @pl.when(jnp.logical_not(p0_self(i)))
        def _():
            p0_copy(i).start()

        @pl.when(p0_self(i))
        def _():
            p0[tm] = starts_v[:, i * BLK : (i + 1) * BLK]

    next_copy = rcopy(starts_v, next_v, next_sem.at[0], next_sem.at[1], ((tm + 15) % 16, row))

    @pl.when(tm > 0)
    def _():
        next_copy.start()

    for i in range(chunks):
        load_a(i).wait()
        high, low = split(a_st[i])
        a_hi[i * rows_a : (i + 1) * rows_a, :] = high
        a_lo[i * rows_a : (i + 1) * rows_a, :] = low

    def x_send(s, d):
        zz = (z + d) % 4
        return rcopy(xb.at[s, z], xb.at[s, z], x_ss.at[s, d], x_rs.at[s, z], at(x, y, zz, c))

    def partner_send(s, zz):
        return rcopy(xb.at[s, zz], xb.at[s, zz], xp_ss.at[s, zz], x_rs.at[s, zz], at(x, y, z, 1 - c))

    def own_block_ready(s):
        for d in range(1, 4):
            x_send(s, d).start()
        partner_send(s, z).start()

    @pl.when(home)
    def _():
        for t in range(16):
            @pl.when(jnp.logical_not((tm == t) & diagonal))
            def _():
                arrived(p0.at[t], p0_ss.at[0], p0_rs.at[t])
        xb[0, z] = p0[...].reshape(LANES, BLK).T
        own_block_ready(0)

    load_l.wait()
    load_r.wait()
    high, low = split(r_v[...])
    r_hi[...] = high
    r_lo[...] = low
    high, low = split(l_v[...].T)
    lt_hi[...] = high
    lt_lo[...] = low
    gpart[...] = (
        dot(lt_hi[...], r_hi[...]) + dot(lt_hi[...], r_lo[...]) + dot(lt_lo[...], r_hi[...])
    ).reshape(gpart.shape)

    def g1_send(d):
        rr = (row + d) % 8
        return rcopy(gpart.at[rr], grs.at[row], g1_ss.at[d], g1_rs.at[row], (tm, rr))

    def g2_send(d):
        rr = (row + d) % 8
        return rcopy(gown, gmat.at[row], g2_ss.at[d], g2_rs.at[row], (tm, rr))

    for d in range(1, 8):
        g1_send(d).start()

    def x_ready(s):
        @pl.when(home)
        def _():
            for d in range(1, 4):
                zz = (z + d) % 4
                arrived(xb.at[s, zz], x_ss.at[s, d], x_rs.at[s, zz])
                partner_send(s, zz).start()

        @pl.when(jnp.logical_not(home))
        def _():
            for zz in range(4):
                arrived(xb.at[s, zz], x_ss.at[s, 0], x_rs.at[s, zz])

        for zz in range(4):
            high, low = split(xb[s, zz] * FINE_TIME)
            xx[zz * BLK : (zz + 1) * BLK, :LANES] = high
            xx[zz * BLK : (zz + 1) * BLK, LANES:] = low

    def product(i):
        span = pl.ds(pl.multiple_of(i * BLK, BLK), BLK)
        both = dot(a_hi[span, :], xx[...]) + dot(a_lo[span, :], xx[...])
        return both[:, :LANES] + both[:, LANES:]

    def p1_local(i):
        return (2 * c + i // 4) == x

    def p1_send(s, i):
        h, zz = i // 4, i % 4
        return rcopy(qb.at[s, i], p1.at[s, x, zz], p1_ss.at[s, i], p1_rs.at[s, x, zz], at(2 * c + h, y, z, c))

    def p2_local(zz):
        return diagonal & (zz == z)

    def p2_send(s, zz):
        return rcopy(sb.at[s, zz], p2.at[s, y], p2_ss.at[s, zz], p2_rs.at[s, y], at(x, z, zz, c))

    def fine_step(s, carry):
        x_ready(s)

        def block(i, carry):
            value = product(i)

            @pl.when(p1_local(i))
            def _():
                p1[s, x, i % 4] = value

            @pl.when(jnp.logical_not(p1_local(i)))
            def _():
                qb[s, i] = value
                p1_send(s, i).start()

            return carry

        lax.fori_loop(0, 8, block, 0)

        @pl.when(home)
        def _():
            def summed(zz, carry):
                for d in range(1, 4):
                    xs = (x + d) % 4
                    arrived(p1.at[s, xs, zz], p1_ss.at[s, 0], p1_rs.at[s, xs, zz])
                total = (p1[s, 0, zz] + p1[s, 1, zz]) + (p1[s, 2, zz] + p1[s, 3, zz])
                total = total + jnp.where(diagonal, xb[s, zz], 0.0)

                @pl.when(p2_local(zz))
                def _():
                    p2[s, y] = total

                @pl.when(jnp.logical_not(p2_local(zz)))
                def _():
                    sb[s, zz] = total
                    p2_send(s, zz).start()

                return carry

            lax.fori_loop(0, 4, summed, 0)

            for yy in range(4):
                @pl.when(jnp.logical_not(diagonal & (y == yy)))
                def _():
                    arrived(p2.at[s, yy], p2_ss.at[s, 0], p2_rs.at[s, yy])
            xb[s + 1, z] = (p2[s, 0] + p2[s, 1]) + (p2[s, 2] + p2[s, 3])
            own_block_ready(s + 1)

        return carry

    lax.fori_loop(0, FINE - 1, fine_step, 0)

    for d in range(1, 8):
        rr = (row + d) % 8
        arrived(grs.at[rr], g1_ss.at[d], g1_rs.at[rr])
    total = gpart[row]
    for d in range(1, 8):
        total = total + grs[(row + d) % 8]
    gown[...] = total
    gmat[row] = total
    for d in range(1, 8):
        g2_send(d).start()
    for d in range(1, 8):
        rr = (row + d) % 8
        arrived(gmat.at[rr], g2_ss.at[d], g2_rs.at[rr])
    rank = gmat.shape[2]
    unit = (
        lax.broadcasted_iota(jnp.int32, (rank, rank), 0) == lax.broadcasted_iota(jnp.int32, (rank, rank), 1)
    ).astype(F32)
    kpow[0] = unit + STEP_TIME * gmat[...].reshape(rank, rank)
    for i in range(3):
        kpow[i + 1] = exact(kpow[i], kpow[i])

    last = FINE - 1
    x_ready(last)
    later = [((tm <= n) & (tm > 0)).astype(F32) for n in range(SLICES)]
    own_block = (diagonal & home).astype(F32)

    def last_block(i, carry):
        value = product(i)
        mine = own_block * ((i // 4) == (x % 2)).astype(F32)
        value = value + mine * xb[last, i % 4]
        turned = value.T.reshape(SLICES, E, BLK)
        span = pl.ds(pl.multiple_of(i * BLK, BLK), BLK)
        base = starts_v[:, span]
        running = turned[0]
        qf[0, 0, :, span] = running - later[0] * base
        for n in range(1, SLICES):
            running = running + turned[n]
            qf[n // 4, n % 4, :, span] = running - later[n] * base
        return carry

    lax.fori_loop(0, 8, last_block, 0)

    def fx_send(d):
        xs = (x + d) % 4
        return rcopy(qf.at[:, xs], fx.at[x], fx_ss.at[d], fx_rs.at[x], at(xs, y, z, c))

    def fy_send(d):
        ys = (y + d) % 4
        return rcopy(fs.at[ys], fy.at[y], fy_ss.at[d], fy_rs.at[y], at(x, ys, z, c))

    for d in range(1, 4):
        fx_send(d).start()
    for d in range(1, 4):
        xs = (x + d) % 4
        arrived(fx.at[xs], fx_ss.at[d], fx_rs.at[xs])
    for d in range(4):
        ys = (y + d) % 4
        fs[ys] = (qf[ys, x] + fx[(x + 1) % 4, ys]) + (fx[(x + 2) % 4, ys] + fx[(x + 3) % 4, ys])
    for d in range(1, 4):
        fy_send(d).start()
    for d in range(1, 4):
        ys = (y + d) % 4
        arrived(fy.at[ys], fy_ss.at[d], fy_rs.at[ys])
    total = (fs[y] + fy[(y + 1) % 4]) + (fy[(y + 2) % 4] + fy[(y + 3) % 4])
    fy[y] = total

    @pl.when(tm < 15)
    def _():
        arrived(next_v, next_sem.at[0], next_sem.at[1])

    @pl.when(tm == 15)
    def _():
        next_v[...] = jnp.zeros_like(next_v)

    high, low = split(total - next_v[...])
    hpart[...] = dot(high, r_hi[...]) + dot(high, r_lo[...]) + dot(low, r_hi[...])

    def h1_send(d):
        rr = (row + d) % 8
        return rcopy(hpart, hrow.at[row], h1_ss.at[d], h1_rs.at[row], (tm, rr))

    def h2_send(d):
        tt = (tm + d) % 16
        return rcopy(hown, hall.at[tm + 1], h2_ss.at[d], h2_rs.at[tm], (tt, row))

    for d in range(1, 8):
        h1_send(d).start()
    for d in range(1, 8):
        rr = (row + d) % 8
        arrived(hrow.at[rr], h1_ss.at[d], h1_rs.at[rr])
    hrow[row] = hpart[...]
    total = hrow[0]
    for i in range(1, 8):
        total = total + hrow[i]
    hown[...] = total
    hall[tm + 1] = total
    hall[0] = jnp.zeros_like(total)
    for d in range(1, 16):
        h2_send(d).start()
    for d in range(1, 16):
        tt = (tm + d) % 16
        arrived(hall.at[tt + 1], h2_ss.at[d], h2_rs.at[tt])
    values = hall[0:SLICES].reshape(LANES, rank)
    for i in range(4):
        shift = E << i
        moved = jnp.concatenate([jnp.zeros((shift, rank), F32), values[: LANES - shift]], axis=0)
        values = values + exact(moved, kpow[i])
    scan[...] = values.reshape(scan.shape)
    high, low = split(scan[tm] * STEP_TIME)
    spread = dot(high, lt_hi[...]) + dot(high, lt_lo[...]) + dot(low, lt_hi[...])
    out_ref[0] = fy[y] + spread

    for i in range(8):
        @pl.when(jnp.logical_not(p0_self(i)))
        def _():
            p0_copy(i).wait_send()

    @pl.when(tm > 0)
    def _():
        next_copy.wait_send()

    for d in range(1, 8):
        g1_send(d).wait_send()
        g2_send(d).wait_send()
        h1_send(d).wait_send()
    for d in range(1, 4):
        fx_send(d).wait_send()
        fy_send(d).wait_send()
    for d in range(1, 16):
        h2_send(d).wait_send()

    @pl.when(home)
    def _():
        def drain(s, carry):
            for d in range(1, 4):
                x_send(s, d).wait_send()
            for zz in range(4):
                partner_send(s, zz).wait_send()
            return carry

        lax.fori_loop(0, FINE, drain, 0)

        def drain_sums(s, carry):
            for zz in range(4):
                @pl.when(jnp.logical_not(p2_local(zz)))
                def _():
                    p2_send(s, zz).wait_send()
            return carry

        lax.fori_loop(0, FINE - 1, drain_sums, 0)

    def drain_products(s, carry):
        for i in range(8):
            @pl.when(jnp.logical_not(p1_local(i)))
            def _():
                p1_send(s, i).wait_send()
        return carry

    lax.fori_loop(0, FINE - 1, drain_products, 0)


def local(starts, operator, coarse_left, coarse_right):
    rows_here, width = operator.shape
    rank = coarse_right.shape[1]
    steps = FINE - 1
    dma = pltpu.SemaphoreType.DMA
    vmem = pltpu.VMEM
    scratch = [
        vmem((E, rows_here), F32),
        vmem((E, rows_here), F32),
        vmem((8, rows_here // 8, width), F32),
        vmem((rows_here, width), BF16),
        vmem((rows_here, width), BF16),
        vmem((rows_here, rank), F32),
        vmem((rows_here, rank), F32),
        vmem((rows_here, rank), BF16),
        vmem((rows_here, rank), BF16),
        vmem((rank, rows_here), BF16),
        vmem((rank, rows_here), BF16),
        vmem((SLICES, E, BLK), F32),
        vmem((FINE, 4, BLK, LANES), F32),
        vmem((width, 2 * LANES), BF16),
        vmem((steps, 8, BLK, LANES), F32),
        vmem((steps, 4, 4, BLK, LANES), F32),
        vmem((steps, 4, BLK, LANES), F32),
        vmem((steps, 4, BLK, LANES), F32),
        vmem((4, 4, E, rows_here), F32),
        vmem((4, 4, E, rows_here), F32),
        vmem((4, E, rows_here), F32),
        vmem((4, E, rows_here), F32),
        vmem((8, rank // 8, rank), F32),
        vmem((8, rank // 8, rank), F32),
        vmem((rank // 8, rank), F32),
        vmem((8, rank // 8, rank), F32),
        vmem((4, rank, rank), F32),
        vmem((E, rank), F32),
        vmem((8, E, rank), F32),
        vmem((E, rank), F32),
        vmem((SLICES + 1, E, rank), F32),
        vmem((SLICES, E, rank), F32),
        dma((11,)),
        dma((2,)),
        dma((8,)), dma((16,)),
        dma((steps, 8)), dma((steps, 4, 4)),
        dma((steps, 4)), dma((steps, 4)),
        dma((FINE, 4)), dma((FINE, 4)), dma((FINE, 4)),
        dma((4,)), dma((4,)), dma((4,)), dma((4,)),
        dma((8,)), dma((8,)), dma((8,)), dma((8,)),
        dma((8,)), dma((8,)), dma((16,)), dma((16,)),
    ]
    return pl.pallas_call(
        kernel,
        out_shape=jax.ShapeDtypeStruct(starts.shape, F32),
        in_specs=[pl.BlockSpec(memory_space=pl.ANY)] * 4,
        out_specs=pl.BlockSpec(memory_space=pltpu.VMEM),
        scratch_shapes=scratch,
        compiler_params=pltpu.CompilerParams(
            collective_id=0, has_side_effects=True, vmem_limit_bytes=63 * 1024 * 1024
        ),
    )(starts, operator, coarse_left, coarse_right)


def solution(mesh):
    in_specs = (P("tm", None, "row"), P("row", "tm"), P("row", None), P("row", None))
    out_specs = P("tm", None, "row")
    return jax.shard_map(local, mesh=mesh, in_specs=in_specs, out_specs=out_specs, check_vma=False)
```

time: 624 us -> 152 us (0.24)
  waiting for transfers between devices: 342 us -> 0 us
  Pallas kernels: 0 us -> 148 us
  blocking collectives: 88.1 us -> 0 us
  starting transfers between devices: 77.9 us -> 0 us
  matrix products: 64.7 us -> 0 us
  local copies, waits for them, and re-layouts: 19.6 us -> 1.47 us
  other arithmetic: 14.9 us -> 0 us
  between operations: 14.7 us -> 0.01 us
    all_gather x5 -> x0, waiting for transfers between devices: 151 us -> none  [broadcast(): lax.all_gather(array, axis)]
    pallas_call x0 -> x1, Pallas kernels: none -> 148 us  [local(): pl.pallas_call(kernel, out_shape=jax.ShapeDtypeStruct(starts.shape, F32),...]
    all_to_all x8 -> x0, waiting for transfers between devices: 98.2 us -> none  [copy_for_each(): lax.all_to_all(jnp.broadcast_to(array[None], (peers, *array.shape)), axis...]
    ppermute x16 -> x0, waiting for transfers between devices: 92.5 us -> none  [shifted(): return lax.ppermute(block, axis, route)]
    all_to_all x4 -> x0, blocking collectives: 88.1 us -> none  [sent_and_summed(): lax.all_to_all(in_blocks(array, dim, peers), axis, 0, 0, tiled=True)]
    dot_general x26 -> x0, matrix products: 64.7 us -> none  [the longest x4 44.6 us: times_columns(): lax.dot_general(vectors, operator, (((1,), (1,)), ((), ())), precision=hi...]
    all_to_all x8 -> x0, starting transfers between devices: 46.6 us -> none  [copy_for_each(): lax.all_to_all(jnp.broadcast_to(array[None], (peers, *array.shape)), axis...]
    ppermute x16 -> x0, starting transfers between devices: 31.2 us -> none  [shifted(): return lax.ppermute(block, axis, route)]
  transfers between devices with their start and end apart: 29 -> 0, of which waited for: 27 -> 0; matrix products, arithmetic and copies ran while one was open for 3% -> 0% of each run, Pallas kernels for 0% -> 0%
where the time goes in v1:
time: 152 us; the launch traced here: 150 us
  Pallas kernels  148 us (97%)
    pallas_call x1, Pallas kernels, local(): pl.pallas_call(kernel, out_shape=jax.ShapeDtypeStruct(starts.shape, F32),...  148 us

profile of v1, /device:TPU:8, one launch (start us, length us, event | category | flops | bytes accessed | tf_op | source)
XLA Modules:
  0.0 150.0 jit_solution(9230289340066310817)
XLA Ops:
  0.0 148.5 %shard_map.46 = f32[1,8,2048]{2,1,0:T(8,128)} custom-call(f32[1,8,2048]{2,1,0:T(8,128)} %starts_hbm.1, f32[2048,1024]{1,0:T(8,128)} %a_hbm.1, f32[2048,256]{1,0:T(8,128)} %l_hbm.1, f32[2048,256]{1,0:T(8,128)} %r_hbm.1), custom_call_target="tpu_custom_call" | custom-call | tf_op jit(solution)/shard_map/pallas_call | solution.py:478
  148.5 1.5 copy.6
